TPU v7x, 32 devices: a whole 2x2x4 slice. The times are simulated.
32 devices in a mesh: dp: 8 (over y, x, core), mp: 4 (over z).
Axes of the slice: x: 2, y: 2, z: 4, core: 2. Of those that a mesh axis runs over, the one named last changes fastest.
Arguments:
- grad_parts: bfloat16 [8, 4, 1024, 4096], P('dp', None, None, 'mp'), may hold values from -4000 to 4000
- master: float32 [4, 1024, 4096], P(None, 'dp', 'mp'), may hold values from -6 to 6
- first_moment: float32 [4, 1024, 4096], P(None, 'dp', 'mp'), may hold values from -4 to 4
- second_moment: float32 [4, 1024, 4096], P(None, 'dp', 'mp'), may hold values from 0.25 to 4
- left_basis: bfloat16 [4, 1024, 4096], P(None, 'dp', 'mp'), may hold values from -1 to 1, as said below
- right_basis: bfloat16 [4, 1024, 4096], P(None, 'dp', 'mp'), may hold values from -1 to 1, as said below
Outputs:
- weights: bfloat16 [4, 1024, 4096], P(None, None, 'mp')
- new_master: float32 [4, 1024, 4096], P(None, 'dp', 'mp')
- new_first: float32 [4, 1024, 4096], P(None, 'dp', 'mp')
- new_second: float32 [4, 1024, 4096], P(None, 'dp', 'mp')
Inputs may be any that keep to these rules, and one draw needn't show every extreme that they name: Each block left_basis[i, :, j * 1024 : (j + 1) * 1024] is an orthogonal 1024 x 1024 matrix up to rounding. Each block right_basis[i, :, j * 1024 : (j + 1) * 1024] is an orthogonal 1024 x 1024 matrix up to rounding.
All inputs are finite; a program needn't handle non-finite values.
Results may differ from a plain program's by a relative error of at most 0.02.
Values may be sent and summed in bfloat16 or wider, within the bound.
A program may use at most 128 MiB of HBM per device.

v0:
```python
import jax
import jax.numpy as jnp
from jax import lax
from jax.sharding import PartitionSpec as P

D = 4096
STEP = 10


beta_one = 0.95
beta_two = 0.95
epsilon = 1e-08
norm_epsilon = 1e-06
learning_rate = 0.3
decay_rate = 0.1


def per_device(grad_parts, master, first_moment, second_moment, left_basis, right_basis):
    gradient = lax.psum_scatter(grad_parts[0], "dp", scatter_dimension=1, tiled=True).astype(
        jnp.float32
    )
    squares_sum = lax.psum(jnp.sum(gradient * gradient), ("dp", "mp"))
    clip_scale = jnp.minimum(1.0, 2.0 * D / jnp.sqrt(squares_sum + norm_epsilon))
    grad_low = gradient.astype(jnp.bfloat16)
    right_full = lax.all_gather(right_basis, "dp", axis=1, tiled=True)
    turned = jnp.einsum(
        "isk,ikb->isb", grad_low, right_full, preferred_element_type=jnp.float32
    ).astype(jnp.bfloat16)
    left_cols = left_basis
    raw_term = jnp.einsum("isx,isb->xib", left_cols, turned, preferred_element_type=jnp.float32)
    rotated_rows = lax.psum_scatter(
        lax.optimization_barrier(raw_term.astype(jnp.bfloat16))
        .astype(jnp.float32)
        .astype(jnp.bfloat16),
        "dp",
        scatter_dimension=0,
        tiled=True,
    ).astype(jnp.float32)
    rotated = jnp.transpose(rotated_rows, (1, 0, 2))
    clipped = clip_scale * rotated
    new_first = beta_one * first_moment + (1.0 - beta_one) * clipped
    new_second = beta_two * second_moment + (1.0 - beta_two) * clipped * clipped
    bias_one = 1.0 - beta_one**STEP
    bias_two = 1.0 - beta_two**STEP
    direction = (new_first / bias_one / (jnp.sqrt(new_second / bias_two) + epsilon)).astype(
        jnp.bfloat16
    )
    back_rows = jnp.einsum(
        "isb,icb->isc", direction, right_full, preferred_element_type=jnp.float32
    ).astype(jnp.bfloat16)
    left_cols = left_basis
    update = jnp.einsum(
        "isk,ikc->isc",
        left_cols,
        lax.all_gather(back_rows, "dp", axis=1, tiled=True),
        preferred_element_type=jnp.float32,
    )
    new_master = master * (1.0 - learning_rate * decay_rate) - learning_rate * update
    weights = lax.all_gather(new_master.astype(jnp.bfloat16), "dp", axis=1, tiled=True)
    return (weights, new_master, new_first, new_second)


def solution(mesh):
    return jax.shard_map(
        per_device,
        mesh=mesh,
        in_specs=(
            P("dp", None, None, "mp"),
            P(None, "dp", "mp"),
            P(None, "dp", "mp"),
            P(None, "dp", "mp"),
            P(None, "dp", "mp"),
            P(None, "dp", "mp"),
        ),
        out_specs=(
            P(None, None, "mp"),
            P(None, "dp", "mp"),
            P(None, "dp", "mp"),
            P(None, "dp", "mp"),
        ),
        check_vma=False,
    )
```

profile of v0, /device:TPU:0, one launch (start us, length us, event | category | flops | bytes accessed | tf_op | source)
XLA Modules:
  0.0 386.3 jit_solution(4198887484840549487)
XLA Ops:
  7.2 0.0 copy-start
  7.2 0.0 reduce-scatter.5.cloned.1.call-start
  7.2 0.7 reduce-scatter.5.cloned.1.call-update
  7.9 0.0 all-gather.4.cloned.1.call-start
  8.0 0.7 all-gather.4.cloned.1.call-update
  8.7 0.0 reduce-scatter.7.cloned.1.call-start
  8.7 77.0 %reduce-scatter.5.cloned.1.call-done = bf16[4,128,1024]{2,1,0:T(8,128)(2,1)} async-done(((bf16[4,1024,1024]{2,1,0:T(8,128)(2,1)}), bf16[4,128,1024]{2,1,0:T(8,128)(2,1)}) %reduce-scatter.5.cloned.1.call-update) | async-done | bytes 1048592 | tf_op jit(solution)/shard_map/reduce_scatter | solution.py:19
  85.7 56.2 %all-gather.4.cloned.1.call-done = bf16[4,1024,1024]{2,1,0:T(8,128)(2,1)} async-done(((bf16[4,128,1024]{2,1,0:T(8,128)(2,1)}), bf16[4,1024,1024]{2,1,0:T(8,128)(2,1)}) %all-gather.4.cloned.1.call-update) | async-done | bytes 8388624 | tf_op jit(solution)/shard_map/all_gather | solution.py:25
  141.9 0.0 copy-done
  141.9 9.2 %convert_bitcast_fusion = bf16[1024,4,1024]{0,2,1:T(8,128)(2,1)} fusion(bf16[4,128,1024]{2,1,0:T(8,128)(2,1)S(1)} %copy-done, bf16[4,128,1024]{2,1,0:T(8,128)(2,1)} %reduce-scatter.5.cloned.1.call-done, bf16[4,1024,1024]{2,1,0:T(8,128)(2,1)} %all-gather.4.cloned.1.call-done), kind=kOutput, calls=%fused_computation | convolution fusion | flops 2152202240 | bytes 18874368 | tf_op jit(solution)/shard_map/isx,isb->xib/dot_general | solution.py:30
  151.1 11.8 %copy.26 = bf16[1024,4096]{1,0:T(8,128)(2,1)} copy(bf16[1024,4096]{0,1:T(8,128)(2,1)} %bitcast.17) | data formatting | bytes 16777216
  162.9 0.0 reduce-scatter.7.cloned.1.call-update
  162.9 0.0 all-gather.6.cloned.1.call-start
  162.9 1.9 copy.18
  164.8 2.4 multiply_reduce_fusion
  167.2 3.3 copy.19
  170.5 39.7 %psum.7 = f32[]{:T(128)} all-reduce(f32[]{:T(128)} %multiply_reduce_fusion), channel_id=1, replica_groups=mesh['dp'=8,'mp'=4] {'dp','mp'}, use_global_device_ids=true, to_apply=%region_2.0 | all-reduce | flops 1 | bytes 8 | tf_op jit(solution)/shard_map/psum | solution.py:22
  210.9 24.3 %reduce-scatter.7.cloned.1.call-done = bf16[128,4096]{1,0:T(8,128)(2,1)} async-done(((bf16[1024,4096]{1,0:T(8,128)(2,1)}), bf16[128,4096]{1,0:T(8,128)(2,1)}) %reduce-scatter.7.cloned.1.call-update) | async-done | bytes 1048592
  235.2 2.3 copy.27
  237.5 2.5 multiply_add_fusion
  239.9 0.0 copy-start.1
  240.0 0.0 copy-start.2
  240.0 1.3 copy-done.1
  241.3 0.7 copy-done.2
  242.0 0.0 copy-start.3
  242.0 7.0 %convolution_convert_fusion = bf16[4,128,1024]{1,2,0:T(8,128)(2,1)} fusion(bf16[4,1024,1024]{2,1,0:T(8,128)(2,1)} %all-gather.4.cloned.1.call-done, f32[4,128,1024]{1,2,0:T(8,128)S(1)} %get-tuple-element.13, f32[4,128,1024]{1,2,0:T(8,128)S(1)} %get-tuple-element.12), kind=kOutput, calls=%fused_computation.8 | convolution fusion | flops 1076887552 | bytes 13631488 | tf_op jit(solution)/shard_map/isb,icb->isc/dot_general | solution.py:48
  249.0 0.0 all-gather.6.cloned.1.call-update
  249.0 0.0 all-gather.8.cloned.1.call-start
  249.0 0.0 copy-done.3
  249.0 1.8 copy.17
  250.9 54.1 %all-gather.6.cloned.1.call-done = bf16[4,1024,1024]{1,2,0:T(8,128)(2,1)} async-done(((bf16[4,128,1024]{1,2,0:T(8,128)(2,1)}), bf16[4,1024,1024]{1,2,0:T(8,128)(2,1)}) %all-gather.6.cloned.1.call-update) | async-done | bytes 8388624 | tf_op jit(solution)/shard_map/all_gather | solution.py:55
  305.0 7.4 %fusion.5 = (bf16[4,128,1024]{1,2,0:T(8,128)(2,1)}, f32[4,128,1024]{1,2,0:T(8,128)S(1)}) fusion(bf16[4,1024,1024]{1,2,0:T(8,128)(2,1)} %all-gather.6.cloned.1.call-done, bf16[4,128,1024]{2,1,0:T(8,128)(2,1)S(1)} %copy-done, f32[4,128,1024]{1,2,0:T(8,128)} %copy.17), kind=kOutput, calls=%fused_computation.14 | convolution fusion | flops 1075838976 | bytes 14680064 | tf_op jit(solution)/shard_map/isk,ikc->isc/dot_general | solution.py:52
  312.4 0.0 all-gather.8.cloned.1.call-update
  312.4 2.9 copy.22
  315.3 2.9 copy.23
  318.2 1.8 copy.21
  320.0 48.4 %all-gather.8.cloned.1.call-done = bf16[4,1024,1024]{1,2,0:T(8,128)(2,1)} async-done(((bf16[4,128,1024]{1,2,0:T(8,128)(2,1)}), bf16[4,1024,1024]{1,2,0:T(8,128)(2,1)}) %all-gather.8.cloned.1.call-update) | async-done | bytes 8388624 | tf_op jit(solution)/shard_map/all_gather | solution.py:59
  368.4 11.3 %copy.20 = bf16[4,1024,1024]{2,1,0:T(8,128)(2,1)} copy(bf16[4,1024,1024]{1,2,0:T(8,128)(2,1)} %all-gather.8.cloned.1.call-done) | data formatting | bytes 16777216
Async XLA Ops:
  7.2 134.7 %copy-start = (bf16[4,128,1024]{2,1,0:T(8,128)(2,1)S(1)}, bf16[4,128,1024]{2,1,0:T(8,128)(2,1)}, u32[]{:S(2)}) copy-start(bf16[4,128,1024]{2,1,0:T(8,128)(2,1)} %param.10) | copy-start | bytes 3145732
  7.2 78.5 %reduce-scatter.5.cloned.1.call-start = ((), (), s32[]{:S(2)}) async-start(), calls=%async_computation.2 | async-start | bytes 9437184 | tf_op jit(solution)/shard_map/reduce_scatter | solution.py:19
  7.9 134.0 %all-gather.4.cloned.1.call-start = ((), (), s32[]{:S(2)}) async-start(), calls=%async_computation.3 | async-start | bytes 9437184 | tf_op jit(solution)/shard_map/all_gather | solution.py:25
  8.7 226.6 %reduce-scatter.7.cloned.1.call-start = ((), (), s32[]{:S(2)}) async-start(), calls=%async_computation.6 | async-start | bytes 9437184
  162.9 142.1 %all-gather.6.cloned.1.call-start = ((), (), s32[]{:S(2)}) async-start(), calls=%async_computation.4 | async-start | bytes 9437184 | tf_op jit(solution)/shard_map/all_gather | solution.py:55
  239.9 1.3 copy-start.1
  240.0 2.0 copy-start.2
  242.0 7.1 %copy-start.3 = (f32[4,128,1024]{2,1,0:T(8,128)S(1)}, f32[4,128,1024]{2,1,0:T(8,128)}, u32[]{:S(2)}) copy-start(f32[4,128,1024]{2,1,0:T(8,128)} %param.7) | copy-start | bytes 6291460
  249.0 119.5 %all-gather.8.cloned.1.call-start = ((), (), s32[]{:S(2)}) async-start(), calls=%async_computation.5 | async-start | bytes 9437184 | tf_op jit(solution)/shard_map/all_gather | solution.py:59
Sparse Core Ops, SparseCore 0:
  11.4 74.2 reduce-scatter.4
  87.6 54.2 all-gather.3
  163.0 72.1 reduce-scatter.6
  249.1 55.8 all-gather.5
  312.5 55.8 all-gather.7
where the time goes:
time: 387 us; the launch traced here: 386 us
  waiting for transfers between devices  262 us (68%)
  local copies, waits for them, and re-layouts  41.9 us (11%)
  blocking collectives  39.7 us (10%)
  matrix products  23.6 us (6%)
  between operations  14.5 us (4%)
  other arithmetic  4.83 us (1%)
    reduce_scatter x1, waiting for transfers between devices, per_device(): lax.psum_scatter(grad_parts[0], 'dp', scatter_dimension=1, tiled=True)  77 us
    all_gather x1, waiting for transfers between devices, per_device(): right_full = lax.all_gather(right_basis, 'dp', axis=1, tiled=True)  56.2 us
    all_gather x1, waiting for transfers between devices, per_device(): lax.all_gather(back_rows, 'dp', axis=1, tiled=True)  54.1 us
    all_gather x1, waiting for transfers between devices, per_device(): lax.all_gather(new_master.astype(jnp.bfloat16), 'dp', axis=1, tiled=True)  48.4 us
    unnamed x17, local copies, waits for them, and re-layouts  41.9 us
    psum x1, blocking collectives, per_device(): squares_sum = lax.psum(jnp.sum(gradient * gradient), ('dp', 'mp'))  39.7 us
    unnamed x6, waiting for transfers between devices  25.7 us
    dot_general x1, matrix products, per_device(): jnp.einsum('isx,isb->xib', left_cols, turned, preferred_element_type=jnp....  9.19 us
  transfers between devices with their start and end apart: 5, of which 5 were waited for; matrix products, arithmetic and copies ran while one was open for 4% of the time, Pallas kernels for 0%

commit v1 on v0

v1 whole, which is shorter than its diff:
```python
import functools

import jax
import jax.numpy as jnp
from jax import lax
from jax.experimental import pallas as pl
from jax.experimental.pallas import tpu as pltpu
from jax.sharding import PartitionSpec as P

D = 4096
STEP = 10


beta_one = 0.95
beta_two = 0.95
epsilon = 1e-08
norm_epsilon = 1e-06
learning_rate = 0.3
decay_rate = 0.1

VMEM = pl.BlockSpec(memory_space=pltpu.VMEM)
MESH = pl.DeviceIdType.MESH


def remote(src, dst, send, recv, axis, index):
    return pltpu.make_async_remote_copy(
        src_ref=src,
        dst_ref=dst,
        send_sem=send,
        recv_sem=recv,
        device_id={axis: index},
        device_id_type=MESH,
    )


def enter(axes):
    barrier = pltpu.get_barrier_semaphore()
    total = 0
    for axis, size in axes:
        me = lax.axis_index(axis)
        for step in range(1, size):
            pl.semaphore_signal(
                barrier,
                inc=1,
                device_id={axis: lax.rem(me + step, size)},
                device_id_type=MESH,
            )
        total += size - 1
    pl.semaphore_wait(barrier, total)


class Gather:
    def __init__(self, n, nb, x, y, local, first, recv, second):
        self.n, self.nb, self.q = n, nb, n // nb
        self.x, self.y = x, y
        self.local, self.first, self.recv, self.second = local, first, recv, second
        self.me = lax.axis_index("dp")
        self.g, self.r = self.me // self.q, lax.rem(self.me, self.q)
        self.sent = []

    def go(self, src, slot, send, target):
        copy = remote(src, self.y.at[slot], send, self.recv.at[slot], "dp", target)
        copy.start()
        self.sent.append(copy)

    def arrived(self, slot):
        remote(
            self.y.at[slot], self.y.at[slot], self.first.at[0], self.recv.at[slot], "dp", self.me
        ).wait_recv()

    def start(self):
        nb, q, me, g, r = self.nb, self.q, self.me, self.g, self.r
        for j in range(1, nb):
            other = lax.rem(g + j, nb)
            self.go(self.x.at[other], me, self.first.at[j], other * q + r)
        for p in range(1, q):
            self.go(self.x.at[g], me, self.second.at[p], g * q + lax.rem(r + p, q))
        self.own = pltpu.make_async_copy(self.x.at[g], self.y.at[me], self.local.at[0])
        self.own.start()

    def forward(self):
        nb, q, g, r = self.nb, self.q, self.g, self.r
        for j in range(1, nb):
            slot = lax.rem(g + nb - j, nb) * q + r
            self.arrived(slot)
            for p in range(1, q):
                self.go(
                    self.y.at[slot], slot, self.second.at[j * q + p], g * q + lax.rem(r + p, q)
                )

    def finish(self):
        nb, q, r = self.nb, self.q, self.r
        self.own.wait()
        for p in range(1, q):
            for j in range(nb):
                self.arrived(j * q + lax.rem(r + p, q))
        for copy in self.sent:
            copy.wait_send()

    @staticmethod
    def scratch(n, nb):
        return [
            pltpu.SemaphoreType.DMA((1,)),
            pltpu.SemaphoreType.DMA((nb,)),
            pltpu.SemaphoreType.DMA((n,)),
            pltpu.SemaphoreType.DMA((n,)),
        ]


class Exchange:
    def __init__(self, n, nb, to_rows, x, y, local, send, recv):
        q = n // nb
        me = lax.axis_index("dp")
        self.nb, self.x, self.y = nb, x, y
        self.local, self.send, self.recv, self.me = local, send, recv, me
        owner = lax.rem(me, q) * nb
        first = me // nb
        if to_rows:
            self.targets = [owner + k for k in range(nb)]
            self.slot = me // q
            self.sources = [k * q + first for k in range(nb)]
        else:
            self.targets = [k * q + first for k in range(nb)]
            self.slot = lax.rem(me, nb)
            self.sources = [owner + k for k in range(nb)]

    def copy(self, k):
        return remote(
            self.x.at[k],
            self.y.at[self.slot],
            self.send.at[k],
            self.recv.at[self.slot],
            "dp",
            self.targets[k],
        )

    def mine(self, k):
        return pltpu.make_async_copy(self.x.at[k], self.y.at[self.slot], self.local.at[0])

    def start(self):
        for k in range(self.nb):

            @pl.when(self.targets[k] != self.me)
            def _():
                self.copy(k).start()

            @pl.when(self.targets[k] == self.me)
            def _():
                self.mine(k).start()

    def finish(self):
        for k in range(self.nb):

            @pl.when(self.sources[k] != self.me)
            def _():
                remote(
                    self.y.at[k], self.y.at[k], self.send.at[k], self.recv.at[k], "dp", self.me
                ).wait_recv()

            @pl.when(self.targets[k] != self.me)
            def _():
                self.copy(k).wait_send()

            @pl.when(self.targets[k] == self.me)
            def _():
                self.mine(k).wait()

    @staticmethod
    def scratch(nb):
        return [
            pltpu.SemaphoreType.DMA((1,)),
            pltpu.SemaphoreType.DMA((nb,)),
            pltpu.SemaphoreType.DMA((nb,)),
        ]


class Share:
    def __init__(self, axis, size, x, y, local, send, recv):
        self.axis, self.size, self.x, self.y = axis, size, x, y
        self.local, self.send, self.recv = local, send, recv
        self.me = lax.axis_index(axis)

    def copy(self, j):
        return remote(
            self.x,
            self.y.at[self.me],
            self.send.at[j],
            self.recv.at[self.me],
            self.axis,
            lax.rem(self.me + j, self.size),
        )

    def start(self):
        for j in range(1, self.size):
            self.copy(j).start()
        self.own = pltpu.make_async_copy(self.x, self.y.at[self.me], self.local.at[0])
        self.own.start()

    def finish(self):
        self.own.wait()
        for j in range(1, self.size):
            slot = lax.rem(self.me + j, self.size)
            remote(
                self.y.at[slot], self.y.at[slot], self.send.at[j], self.recv.at[slot], self.axis, slot
            ).wait_recv()
        for j in range(1, self.size):
            self.copy(j).wait_send()

    @staticmethod
    def scratch(size):
        return [
            pltpu.SemaphoreType.DMA((1,)),
            pltpu.SemaphoreType.DMA((size,)),
            pltpu.SemaphoreType.DMA((size,)),
        ]


def bases_kernel(n, nb, left, right, master, left_out, right_out, master_out, *sems):
    enter([("dp", n)])
    one = Gather(n, nb, right, right_out, *sems[0:4])
    two = Gather(n, nb, left, left_out, *sems[4:8])
    three = Exchange(n, nb, False, master, master_out, *sems[8:11])
    one.start()
    two.start()
    three.start()
    one.forward()
    two.forward()
    one.finish()
    two.finish()
    three.finish()


def gather_kernel(n, nb, x, y, *sems):
    enter([("dp", n)])
    one = Gather(n, nb, x, y, *sems)
    one.start()
    one.forward()
    one.finish()


def scatter_kernel(n, nb, x, y, *sems):
    enter([("dp", n)])
    one = Exchange(n, nb, True, x, y, *sems)
    one.start()
    one.finish()


def scatter_sum_kernel(n, m, nb, x, part, y, parts, *sems):
    enter([("dp", n), ("mp", m)])
    two = Share("mp", m, part, parts, *sems[3:6])
    two.start()
    one = Exchange(n, nb, True, x, y, *sems[0:3])
    one.start()
    two.finish()
    one.finish()


def group_kernel(n, nb, x, part, y, parts, *sems):
    enter([("dp", n)])
    q = n // nb
    me = lax.axis_index("dp")
    g, r = me // q, lax.rem(me, q)
    local, send, recv = sems[0:3]
    copies = []
    for p in range(1, q):
        copy = remote(
            x, y.at[r], send.at[p], recv.at[r], "dp", g * q + lax.rem(r + p, q)
        )
        copy.start()
        copies.append(copy)
    two = Share("dp", n, part, parts, *sems[3:6])
    two.start()
    own = pltpu.make_async_copy(x, y.at[r], local.at[0])
    own.start()
    own.wait()
    for p in range(1, q):
        slot = lax.rem(r + p, q)
        remote(y.at[slot], y.at[slot], send.at[p], recv.at[slot], "dp", me).wait_recv()
    two.finish()
    for copy in copies:
        copy.wait_send()


def call(kernel, shapes, scratch, collective_id, *args):
    moved = sum(s.size * s.dtype.itemsize for s in shapes)
    return pl.pallas_call(
        kernel,
        out_shape=shapes,
        in_specs=[VMEM] * len(args),
        out_specs=[VMEM] * len(shapes),
        scratch_shapes=scratch,
        compiler_params=pltpu.CompilerParams(
            collective_id=collective_id, has_side_effects=True, vmem_limit_bytes=32 * 1024 * 1024
        ),
        cost_estimate=pl.CostEstimate(flops=0, bytes_accessed=16 * moved, transcendentals=0),
    )(*args)


def per_device(n, m, grad_parts, master, first_moment, second_moment, left_basis, right_basis):
    bf16, f32 = jnp.bfloat16, jnp.float32
    nb, rb, cols = master.shape
    blk = rb * n
    q = n // nb
    hb = blk // q
    r = lax.rem(lax.axis_index("dp"), q)
    pieces = jax.ShapeDtypeStruct((nb, rb, cols), bf16)
    block = jax.ShapeDtypeStruct((n, rb, cols), bf16)
    low_sum = lax.psum_scatter(
        grad_parts.reshape(nb * blk, cols), "dp", scatter_dimension=0, tiled=True
    )
    left, right, master_low = call(
        functools.partial(bases_kernel, n, nb),
        [block, block, pieces],
        Gather.scratch(n, nb) * 2 + Exchange.scratch(nb),
        0,
        left_basis,
        right_basis,
        master.astype(bf16),
    )
    left, right = left.reshape(blk, cols), right.reshape(blk, cols)
    left_cols = lax.dynamic_slice_in_dim(left, r * hb, hb, axis=1)
    left_rows = lax.dynamic_slice_in_dim(left, r * hb, hb, axis=0)
    gradient = low_sum.astype(f32)
    part = jnp.full((8, 128), jnp.sum(gradient * gradient), f32)
    grad_block, parts = call(
        functools.partial(group_kernel, n, nb),
        [
            jax.ShapeDtypeStruct((q, hb, cols), bf16),
            jax.ShapeDtypeStruct((n, 8, 128), f32),
        ],
        Share.scratch(q) + Share.scratch(n),
        1,
        low_sum,
        part,
    )
    part = jnp.sum(parts, axis=0)
    turned = jnp.dot(
        grad_block.reshape(blk, cols), right, preferred_element_type=f32
    ).astype(bf16)
    rotated_rows = lax.dot_general(
        left_cols, turned, (((0,), (0,)), ((), ())), preferred_element_type=f32
    ).astype(bf16)
    rotated, parts = call(
        functools.partial(scatter_sum_kernel, n, m, nb),
        [pieces, jax.ShapeDtypeStruct((m, 8, 128), f32)],
        Exchange.scratch(nb) + Share.scratch(m),
        2,
        rotated_rows.reshape(nb, rb, cols),
        part,
    )
    squares_sum = jnp.sum(parts[:, 0, 0])
    clip_scale = jnp.minimum(1.0, 2.0 * D / jnp.sqrt(squares_sum + norm_epsilon))
    clipped = clip_scale * rotated.astype(f32)
    new_first = beta_one * first_moment + (1.0 - beta_one) * clipped
    new_second = beta_two * second_moment + (1.0 - beta_two) * clipped * clipped
    bias_one = 1.0 - beta_one**STEP
    bias_two = 1.0 - beta_two**STEP
    direction = (new_first / bias_one / (jnp.sqrt(new_second / bias_two) + epsilon)).astype(bf16)
    (direction_block,) = call(
        functools.partial(gather_kernel, n, nb), [block], Gather.scratch(n, nb), 3, direction
    )
    back = lax.dot_general(
        direction_block.reshape(blk, cols),
        right,
        (((1,), (1,)), ((), ())),
        preferred_element_type=f32,
    ).astype(bf16)
    update = jnp.dot(left_rows, back, preferred_element_type=f32)
    keep = 1.0 - learning_rate * decay_rate
    weight_rows = (
        master_low.reshape(hb, cols).astype(f32) * keep - learning_rate * update
    ).astype(bf16)
    weights = lax.all_gather(weight_rows, "dp", axis=0, tiled=True).reshape(nb, blk, cols)
    (update_rows,) = call(
        functools.partial(scatter_kernel, n, nb),
        [pieces],
        Exchange.scratch(nb),
        4,
        update.astype(bf16).reshape(nb, rb, cols),
    )
    new_master = master * keep - learning_rate * update_rows.astype(f32)
    return (weights, new_master, new_first, new_second)


def solution(mesh):
    n, m = mesh.shape["dp"], mesh.shape["mp"]
    return jax.shard_map(
        functools.partial(per_device, n, m),
        mesh=mesh,
        in_specs=(
            P("dp", None, None, "mp"),
            P(None, "dp", "mp"),
            P(None, "dp", "mp"),
            P(None, "dp", "mp"),
            P(None, "dp", "mp"),
            P(None, "dp", "mp"),
        ),
        out_specs=(
            P(None, None, "mp"),
            P(None, "dp", "mp"),
            P(None, "dp", "mp"),
            P(None, "dp", "mp"),
        ),
        check_vma=False,
    )
```

time: 387 us -> 229 us (0.59)
  waiting for transfers between devices: 262 us -> 66.8 us
  Pallas kernels: 0 us -> 106 us
  blocking collectives: 39.7 us -> 0 us
  local copies, waits for them, and re-layouts: 41.9 us -> 13.8 us
  matrix products: 23.6 us -> 13 us
  other arithmetic: 4.83 us -> 13.9 us
    all_gather x3 -> x1, waiting for transfers between devices: 159 us -> 34.9 us  [per_device(): lax.all_gather(weight_rows, 'dp', axis=0, tiled=True).reshape(nb, blk, cols)]
    pallas_call x0 -> x5, Pallas kernels: none -> 106 us  [call(): pl.pallas_call(kernel, out_shape=shapes, in_specs=[VMEM] * len(args), out...]
    reduce_scatter x1, waiting for transfers between devices: 77 us -> 31.3 us  [per_device(): lax.psum_scatter(grad_parts.reshape(nb * blk, cols), 'dp', scatter_dimens...]
    psum x1 -> x0, blocking collectives: 39.7 us -> none  [per_device(): squares_sum = lax.psum(jnp.sum(gradient * gradient), ('dp', 'mp'))]
    unnamed x17 -> x15, local copies, waits for them, and re-layouts: 41.9 us -> 13.2 us
    unnamed x6 -> x2, waiting for transfers between devices: 25.7 us -> 0.7 us
    dot_general x3 -> x2, matrix products: 23.6 us -> 13 us  [the longest x1 7.06 us: per_device(): update = jnp.dot(left_rows, back, preferred_element_type=f32)]
    convert_element_type x0 -> x2, other arithmetic: none -> 7.61 us  [the longest x1 5.73 us: per_device(): (new_first / bias_one / (jnp.sqrt(new_second / bias_two) + epsilon)).asty...]
  transfers between devices with their start and end apart: 5 -> 2, of which waited for: 5 -> 2; matrix products, arithmetic and copies ran while one was open for 4% -> 2% of each run, Pallas kernels for 0% -> 30%
where the time goes in v1:
time: 229 us
  Pallas kernels  106 us (46%)
  waiting for transfers between devices  66.8 us (29%)
  between operations  14.9 us (7%)
  other arithmetic  13.9 us (6%)
  local copies, waits for them, and re-layouts  13.8 us (6%)
  matrix products  13 us (6%)
    pallas_call x5, Pallas kernels, call(): pl.pallas_call(kernel, out_shape=shapes, in_specs=[VMEM] * len(args), out...  106 us
    all_gather x1, waiting for transfers between devices, per_device(): lax.all_gather(weight_rows, 'dp', axis=0, tiled=True).reshape(nb, blk, cols)  34.9 us
    reduce_scatter x1, waiting for transfers between devices, per_device(): lax.psum_scatter(grad_parts.reshape(nb * blk, cols), 'dp', scatter_dimens...  31.3 us
    unnamed x15, local copies, waits for them, and re-layouts  13.2 us
    dot_general x1, matrix products, per_device(): update = jnp.dot(left_rows, back, preferred_element_type=f32)  7.06 us
    dot_general x1, matrix products, per_device(): lax.dot_general(left_cols, turned, (((0,), (0,)), ((), ())), preferred_el...  5.95 us
    convert_element_type x1, other arithmetic, per_device(): (new_first / bias_one / (jnp.sqrt(new_second / bias_two) + epsilon)).asty...  5.73 us
  transfers between devices with their start and end apart: 2, of which 2 were waited for; matrix products, arithmetic and copies ran while one was open for 2% of the time, Pallas kernels for 30%

profile of v1, /device:TPU:0, one launch (start us, length us, event | category | flops | bytes accessed | tf_op | source)
XLA Modules:
  0.0 228.5 jit_solution(6726912487059157967)
XLA Ops:
  7.2 0.0 reduce-scatter.2.cloned.1.call-start
  7.2 0.7 reduce-scatter.2.cloned.1.call-update
  7.9 0.0 copy-start.1
  7.9 0.0 copy-start.2
  7.9 0.0 all-gather.2.cloned.1.call-start
  8.0 1.9 convert_element_type.34.master
  9.9 0.0 copy-done.1
  9.9 0.2 copy-done.2
  10.1 48.1 %shard_map.93 = (bf16[8,128,1024]{2,1,0:T(8,128)(2,1)S(1)}, bf16[8,128,1024]{2,1,0:T(8,128)(2,1)S(1)}, bf16[4,128,1024]{2,1,0:T(8,128)(2,1)S(1)}) custom-call(bf16[4,128,1024]{2,1,0:T(8,128)(2,1)S(1)} %copy-done.1, bf16[4,128,1024]{2,1,0:T(8,128)(2,1)S(1)} %copy-done.2, bf16[4,128,1024]{2,1,0:T(8,128)(2,1)S(1)} %convert_element_type.34.master), custom_call_target="tpu_custom_call" | custom-call | bytes 83886080 | tf_op jit(solution)/shard_map/pallas_call | solution.py:286
  58.1 0.0 copy-start.3
  58.2 1.3 copy-done.3
  59.5 0.0 copy-start.4
  59.5 1.3 copy-done.4
  60.8 1.6 convert_multiply_fusion.1
  62.4 31.3 %reduce-scatter.2.cloned.1.call-done.x = bf16[512,1024]{1,0:T(8,128)(2,1)} async-done(((bf16[4096,1024]{1,0:T(8,128)(2,1)}), bf16[512,1024]{1,0:T(8,128)(2,1)}) %reduce-scatter.2.cloned.1.call-update) | async-done | bytes 1048592 | tf_op jit(solution)/shard_map/reduce_scatter | solution.py:308
  93.7 2.4 %multiply_reduce_fusion = f32[]{:T(128)} fusion(bf16[512,1024]{1,0:T(8,128)(2,1)} %reduce-scatter.2.cloned.1.call-done.x), kind=kLoop, calls=%fused_computation.12 | loop fusion | flops 1572863 | bytes 1048580 | tf_op jit(solution)/shard_map/reduce_sum | solution.py:324
  96.1 0.6 broadcast_in_dim.3.part
  96.7 0.0 copy-start
  96.7 1.2 copy-done
  97.9 4.8 %shard_map.94 = (bf16[2,512,1024]{2,1,0:T(8,128)(2,1)S(1)}, f32[8,8,128]{2,1,0:T(8,128)S(1)}) custom-call(bf16[512,1024]{1,0:T(8,128)(2,1)S(1)} %copy-done, f32[8,128]{1,0:T(8,128)S(1)} %broadcast_in_dim.3.part), custom_call_target="tpu_custom_call" | custom-call | bytes 34078720 | tf_op jit(solution)/shard_map/pallas_call | solution.py:286
  102.7 0.0 copy-start.5
  102.8 1.3 copy-done.5
  104.1 5.9 %fusion.6 = bf16[512,1024]{1,0:T(8,128)(2,1)S(1)} fusion(bf16[1024,1024]{1,0:T(8,128)(2,1)} %bitcast.23, bf16[1024,1024]{1,0:T(8,128)(2,1)} %bitcast.21, bf16[1024,1024]{1,0:T(8,128)(2,1)} %bitcast.19, s32[]{:T(128)S(6)} %select_n.4), kind=kOutput, calls=%fused_computation.14 | convolution fusion | flops 3222798336 | bytes 6291460 | tf_op jit(solution)/shard_map/dot_general | solution.py:340
  110.0 15.1 %shard_map.95 = (bf16[4,128,1024]{2,1,0:T(8,128)(2,1)S(1)}, f32[4,8,128]{2,1,0:T(8,128)S(1)}) custom-call(bf16[4,128,1024]{2,1,0:T(8,128)(2,1)S(1)} %bitcast.18, f32[8,128]{1,0:T(8,128)S(1)} %reduce_sum.28.part), custom_call_target="tpu_custom_call" | custom-call | bytes 17039360 | tf_op jit(solution)/shard_map/pallas_call | solution.py:286
  125.1 0.6 slice_reduce_fusion
  126.4 5.7 %divide_convert_fusion = (bf16[4,128,1024]{2,1,0:T(8,128)(2,1)S(1)}, f32[4,128,1024]{2,1,0:T(8,128)}, f32[4,128,1024]{2,1,0:T(8,128)}) fusion(bf16[4,128,1024]{2,1,0:T(8,128)(2,1)S(1)} %get-tuple-element.17, f32[]{:T(128)S(6)} %min_shard_map.3, f32[4,128,1024]{2,1,0:T(8,128)} %param.8, f32[4,128,1024]{2,1,0:T(8,128)} %param.9), kind=kLoop, calls=%fused_computation.8 | loop fusion | flops 6815744 | bytes 10485764 | tf_op jit(solution)/shard_map/convert_element_type | solution.py:358
  132.1 18.2 %shard_map.96 = bf16[8,128,1024]{2,1,0:T(8,128)(2,1)S(1)} custom-call(bf16[4,128,1024]{2,1,0:T(8,128)(2,1)S(1)} %get-tuple-element.18.x), custom_call_target="tpu_custom_call" | custom-call | bytes 33554432 | tf_op jit(solution)/shard_map/pallas_call | solution.py:286
  150.3 7.1 %fusion.18 = (bf16[512,1024]{1,0:T(8,128)(2,1)S(1)}, bf16[512,1024]{1,0:T(8,128)(2,1)}) fusion(f32[4,128,1024]{2,1,0:T(8,128)} %convert_multiply_fusion.1, bf16[1024,1024]{1,0:T(8,128)(2,1)S(1)} %bitcast.16, bf16[1024,1024]{1,0:T(8,128)(2,1)} %bitcast.22, bf16[1024,1024]{1,0:T(8,128)(2,1)} %bitcast.20, s32[]{:T(128)S(6)} %select_n.4), kind=kOutput, calls=%fused_computation.22 | convolution fusion | flops 3224371200 | bytes 9437188 | tf_op jit(solution)/shard_map/dot_general | solution.py:368
  157.3 0.0 copy-start.6
  157.4 0.0 all-gather.2.cloned.1.call-update
  157.4 20.0 %shard_map.97 = bf16[4,128,1024]{2,1,0:T(8,128)(2,1)S(1)} custom-call(bf16[4,128,1024]{2,1,0:T(8,128)(2,1)S(1)} %bitcast.17), custom_call_target="tpu_custom_call" | custom-call | bytes 16777216 | tf_op jit(solution)/shard_map/pallas_call | solution.py:286
  177.4 0.0 copy-done.6
  177.4 1.7 multiply_subtract_fusion
  179.1 34.9 %all-gather.2.cloned.1.call-done = bf16[4096,1024]{1,0:T(8,128)(2,1)} async-done(((bf16[512,1024]{1,0:T(8,128)(2,1)}), bf16[4096,1024]{1,0:T(8,128)(2,1)}) %all-gather.2.cloned.1.call-update) | async-done | bytes 8388624 | tf_op jit(solution)/shard_map/all_gather | solution.py:373
  213.9 7.8 %copy.11 = bf16[4,1024,1024]{2,1,0:T(8,128)(2,1)} copy(bf16[4,1024,1024]{2,1,0:T(8,128)(2,1)} %bitcast.25) | data formatting | bytes 16777216
  (1 shorter events, 0.0 us)
Async XLA Ops:
  7.2 86.5 %reduce-scatter.2.cloned.1.call-start = ((), (), s32[]{:S(2)}) async-start(), calls=%async_computation.1 | async-start | bytes 9437184 | tf_op jit(solution)/shard_map/reduce_scatter | solution.py:308
  7.9 2.0 copy-start.1
  7.9 2.2 copy-start.2
  7.9 206.0 %all-gather.2.cloned.1.call-start = ((), (), s32[]{:S(2)}) async-start(), calls=%async_computation.2 | async-start | bytes 9437184 | tf_op jit(solution)/shard_map/all_gather | solution.py:373
  58.1 1.4 copy-start.3
  59.5 1.3 copy-start.4
  96.7 1.2 copy-start
  102.7 1.3 copy-start.5
  157.3 20.0 %copy-start.6 = (f32[4,128,1024]{2,1,0:T(8,128)S(1)}, f32[4,128,1024]{2,1,0:T(8,128)}, u32[]{:S(2)}) copy-start(f32[4,128,1024]{2,1,0:T(8,128)} %param.7) | copy-start | bytes 6291460
Sparse Core Ops, SparseCore 0:
  11.4 82.2 reduce-scatter.1
  157.5 56.3 all-gather.1
